TPU v7x, 256 devices: a whole 4x4x8 slice. The times are simulated.
256 devices in a mesh: dp: 64 (over z, y, core), mp: 4 (over x).
Axes of the slice: x: 4, y: 4, z: 8, core: 2. Of those that a mesh axis runs over, the one named last changes fastest.
Arguments:
- patches: bfloat16 [131072, 1024], P('dp'), may hold values from -110 to 110
- dest_owner: int32 [8192], P('dp'), may hold values from 0 to 63, as said below
- dest_slot: int32 [8192], P('dp'), may hold values from 0 to 127
- packed_image: int32 [8192], P('dp'), may hold values from -1 to 15, as said below
- w_query: bfloat16 [1024, 1024], P(None, 'mp'), may hold values from -0.328125 to 0.328125
- w_key: bfloat16 [1024, 1024], P(None, 'mp'), may hold values from -1.9375 to 1.9375
- w_value: bfloat16 [1024, 1024], P(None, 'mp'), may hold values from -0.1875 to 0.1875
- w_out: bfloat16 [1024, 1024], P('mp'), may hold values from -0.1875 to 0.1875
Outputs:
- packed_out: bfloat16 [131072, 1024], P('dp', 'mp')
- pooled_out: bfloat16 [1024, 1024], P('dp', 'mp')
Inputs may be any that keep to these rules, and one draw needn't show every extreme that they name: dest_owner and dest_slot take the tiles of all indices of dp one to one onto the 128 tile slots of every packed sequence; each index of dp holds exactly 2 tiles for each packed sequence. `packed_image`: in every packed sequence the images 0, 1, 2 and so on lie on consecutive tile slots from slot 0 in the order of their numbers, each on 8 to 16 slots; fewer than 16 slots stay empty after the last image and hold -1.
All inputs are finite; a program needn't handle non-finite values.
Results may differ from a plain program's by a relative error of at most 0.0075.
Values may be sent and summed in bfloat16 or wider, within the bound.
No kernel may reach another device: no remote copies, remote signals or barrier semaphores. Data moves between devices by JAX's collectives and lax.ppermute only.
A program may use at most 128 MiB of HBM per device.

v0:
```python
import jax
import jax.numpy as jnp
from jax import lax
from jax.sharding import PartitionSpec as P

HEAD_DIM = 64
IMG_OWN = 16
EPSILON = 1e-06


def cut_along(shard, dim, length):
    lengths = shard.shape
    tiles = shard.reshape(*lengths[:dim], length, lengths[dim] // length, *lengths[dim + 1 :])
    return jnp.moveaxis(tiles, dim, 0)


def sent_and_summed(shard, axis, dim):
    length = lax.axis_size(axis)
    tiles = lax.all_to_all(cut_along(shard, dim, length), axis, 0, 0, tiled=True)
    return jnp.sum(tiles.astype(jnp.float32), axis=0)


def sent_to_all(shard, axis):
    copies = jnp.broadcast_to(shard, (lax.axis_size(axis), *shard.shape))
    return lax.all_to_all(copies, axis, split_axis=0, concat_axis=0, tiled=True)


def of_everyone(shard, axis):
    return sent_to_all(shard, axis).sum(axis=0)


def in_one(arrays, axis):
    line, at, outs = (jnp.concatenate([a.reshape(-1) for a in arrays]), 0, [])
    running = of_everyone(line, axis)
    for a in arrays:
        outs.append(running[at : at + a.size].reshape(a.shape))
        at += a.size
    return tuple(outs)


def normalize(rows):
    values = rows.astype(jnp.float32)
    centred = values - jnp.mean(values, axis=-1, keepdims=True)
    spread = jnp.mean(centred * centred, axis=-1, keepdims=True)
    return (centred * lax.rsqrt(spread + EPSILON)).astype(jnp.bfloat16)


def attend(queries, key_rows, values, allowed, present):
    scores = jnp.einsum(
        "qhd,khd->hqk", queries, key_rows, preferred_element_type=jnp.float32
    ) * HEAD_DIM ** (-0.5)
    masked = jnp.where(allowed[None], scores, -1e30)
    peak = jnp.max(masked, axis=-1, keepdims=True)
    raised = jnp.where(allowed[None], jnp.exp(scores - peak), 0.0)
    denominator = jnp.sum(raised, axis=-1, keepdims=True)
    denominator = jnp.where(present[None, :, None], denominator, 1.0)
    weights = (raised / denominator).astype(jnp.bfloat16)
    return jnp.einsum("hqk,khd->qhd", weights, values, preferred_element_type=jnp.float32).astype(
        jnp.bfloat16
    )


def whole_rows(queries, key_rows, values, segment, present):
    count_rows = queries.shape[0]
    block_rows = min(512, count_rows)

    def one_block(step_index):
        first_row = step_index * block_rows
        query_part = lax.dynamic_slice_in_dim(queries, first_row, block_rows, 0)
        segment_part = lax.dynamic_slice_in_dim(segment, first_row, block_rows, 0)
        live_rows = lax.dynamic_slice_in_dim(present, first_row, block_rows, 0)
        allowed = (segment_part[:, None] == segment[None, :]) & live_rows[:, None]
        return attend(query_part, key_rows, values, allowed, live_rows)

    outcome = lax.map(one_block, jnp.arange(count_rows // block_rows, dtype=jnp.int32))
    return outcome.reshape(count_rows, -1)


def on_device(patches, dest_owner, dest_slot, packed_image, w_query, w_key, w_value, w_out):
    senders = lax.axis_size("dp")
    splits = lax.axis_size("mp")
    slot_count = dest_owner.shape[0]
    per_owner = slot_count // senders
    tile_size = patches.shape[0] // slot_count
    full_width = patches.shape[1]
    part_width = full_width // splits
    numbers = jnp.arange(slot_count, dtype=jnp.int32)
    same_owner = dest_owner[:, None] == dest_owner[None, :]
    ranking = jnp.sum(
        (same_owner & (numbers[None, :] < numbers[:, None])).astype(jnp.int32), axis=1
    )
    position = dest_owner * per_owner + ranking
    picked = position[None, :] == numbers[:, None]
    ordering = jnp.sum(jnp.where(picked, numbers[None, :], 0), axis=1)
    slot_sent = jnp.sum(jnp.where(picked, dest_slot[None, :], 0), axis=1)
    got_slot = lax.all_to_all(slot_sent, "dp", split_axis=0, concat_axis=0, tiled=True)
    arrive = jnp.sum(jnp.where(got_slot[None, :] == numbers[:, None], numbers[None, :], 0), axis=1)
    tile_data = patches.reshape(slot_count, tile_size, full_width)
    column_start = lax.axis_index("mp") * part_width
    own_part = lax.dynamic_slice_in_dim(tile_data, column_start, part_width, 2)
    outgoing = jnp.take(own_part, ordering, axis=0).reshape(slot_count * tile_size, part_width)
    incoming = lax.all_to_all(outgoing, "dp", split_axis=0, concat_axis=0, tiled=True)
    own_cols = jnp.take(
        incoming.reshape(slot_count, tile_size, part_width), arrive, axis=0
    ).reshape(slot_count * tile_size, part_width)
    full_rows = lax.all_gather(own_cols, "mp", axis=1, tiled=True)
    count_rows = slot_count * tile_size
    segment = jnp.repeat(packed_image, tile_size)
    present = segment >= 0
    normed = normalize(full_rows)
    head_count = w_query.shape[1] // HEAD_DIM
    queries = (
        jnp.dot(normed, w_query, preferred_element_type=jnp.float32)
        .astype(jnp.bfloat16)
        .reshape(count_rows, head_count, HEAD_DIM)
    )
    key_rows = (
        jnp.dot(normed, w_key, preferred_element_type=jnp.float32)
        .astype(jnp.bfloat16)
        .reshape(count_rows, head_count, HEAD_DIM)
    )
    values = (
        jnp.dot(normed, w_value, preferred_element_type=jnp.float32)
        .astype(jnp.bfloat16)
        .reshape(count_rows, head_count, HEAD_DIM)
    )
    attended = whole_rows(queries, key_rows, values, segment, present)
    head_term = jnp.dot(attended, w_out, preferred_element_type=jnp.float32)
    summed = sent_and_summed(head_term.astype(jnp.bfloat16), "mp", 1)
    result_rows = jnp.where(present[:, None], own_cols.astype(jnp.float32) + summed, 0.0)
    packed_out = result_rows.astype(jnp.bfloat16)
    labels = jnp.arange(IMG_OWN, dtype=jnp.int32)
    member = (segment[None, :] == labels[:, None]).astype(jnp.float32)
    sums = jnp.dot(member, result_rows)
    image_rows = jnp.sum(member, axis=1)
    filled = image_rows > 0
    pooled = sums / jnp.maximum(image_rows, 1.0)[:, None]
    local_sum = jnp.sum(jnp.where(filled[:, None], pooled, 0.0), axis=0)
    local_count = jnp.sum(filled.astype(jnp.float32))
    grand_total, number = in_one((local_sum, local_count), "dp")
    centre = grand_total / number
    pooled_out = jnp.where(filled[:, None], pooled - centre[None, :], 0.0).astype(jnp.bfloat16)
    return (packed_out, pooled_out)


def solution(mesh):
    in_specs = (
        P("dp", None),
        P("dp"),
        P("dp"),
        P("dp"),
        P(None, "mp"),
        P(None, "mp"),
        P(None, "mp"),
        P("mp", None),
    )
    out_specs = (P("dp", "mp"), P("dp", "mp"))
    return jax.shard_map(
        on_device, mesh=mesh, in_specs=in_specs, out_specs=out_specs, check_vma=False
    )
```

profile of v0, /device:TPU:1, one launch (start us, length us, event | category | flops | bytes accessed | tf_op | source)
XLA Modules:
  0.0 322.7 jit_solution(6817620751752851636)
XLA Ops:
  10.3 13.1 %all-to-all-start.1 = ((s32[64,2,1]{1,2,0:T(1,128)}), s32[64,2,1]{1,2,0:T(1,128)S(1)}, u32[]{:S(2)}, u32[]{:S(2)}) async-start(s32[64,2,1]{1,2,0:T(1,128)} %bitcast), calls=%async_computation.1 | async-start | bytes 65536 | tf_op jit(solution)/shard_map/all_to_all | solution.py:96
  23.5 1.3 constant_dynamic-slice_fusion
  25.4 1.2 broadcast_select_fusion.2
  26.6 6.2 %all-to-all-done.1 = s32[64,2,1]{1,2,0:T(1,128)S(1)} async-done(((s32[64,2,1]{1,2,0:T(1,128)}), s32[64,2,1]{1,2,0:T(1,128)S(1)}, u32[]{:S(2)}, u32[]{:S(2)}) %all-to-all-start.1) | async-done | bytes 544 | tf_op jit(solution)/shard_map/all_to_all | solution.py:96
  32.8 4.7 %all-to-all-start = ((bf16[64,32,256]{2,1,0:T(8,128)(2,1)}), bf16[64,32,256]{2,1,0:T(8,128)(2,1)S(1)}, u32[]{:S(2)}, u32[]{:S(2)}) async-start(bf16[64,32,256]{2,1,0:T(8,128)(2,1)} %bitcast.2), calls=%async_computation | async-start | bytes 2097152 | tf_op jit(solution)/shard_map/all_to_all | solution.py:102
  39.2 26.7 %all-to-all-done = bf16[64,32,256]{2,1,0:T(8,128)(2,1)S(1)} async-done(((bf16[64,32,256]{2,1,0:T(8,128)(2,1)}), bf16[64,32,256]{2,1,0:T(8,128)(2,1)S(1)}, u32[]{:S(2)}, u32[]{:S(2)}) %all-to-all-start) | async-done | bytes 1048608 | tf_op jit(solution)/shard_map/all_to_all | solution.py:102
  66.5 1.2 broadcast_select_fusion.1
  67.9 49.4 %all-gather.2.cloned.1.call-done = bf16[2048,1024]{1,0:T(8,128)(2,1)} async-done(((bf16[2048,256]{1,0:T(8,128)(2,1)}), bf16[2048,1024]{1,0:T(8,128)(2,1)}) %all-gather.2.cloned.1.call-update) | async-done | bytes 4194320 | tf_op jit(solution)/shard_map/all_gather | solution.py:106
  117.4 3.0 convert_reduce_fusion
  120.8 1.4 fusion.31
  122.2 1.1 fusion.32
  123.4 2.3 convolution_convert_fusion.3
  125.7 2.3 convolution_convert_fusion.2
  128.0 2.3 convolution_convert_fusion.1
  130.3 98.7 %while.11 = (s32[]{:T(128)}, bf16[4,512,4,64]{1,3,2,0:T(8,128)(2,1)S(1)}, s32[4]{0:T(128)S(1)}, s32[2048]{0:T(1024)S(1)}, pred[2048]{0:T(1024)(128)(4,1)S(1)}, /...) while((s32[]{:T(128)}, ...), condition=%wide.region_9.11_spmd.clone, body=%wide.region_6.0_spmd.clone.sunk | while | flops 1646399488 | bytes 40707776 | solution.py:75
  132.8 13.4 %fusion.69 = (f32[4,512]{1,0:T(4,128)S(1)}, f32[4,512,2048]{2,1,0:T(8,128)}) fusion(pred[512,2048]{1,0:T(8,128)(4,1)S(1)} %compare_and_fusion.4, bf16[2048,4,64]{0,2,1:T(8,128)(2,1)} %get-tuple-element.197, bf16[2048,4,64]{0,2,1:T(8,128)(2,1)} %get-tuple-element.196, s32[]{:T(128)S(6)} %select_n.104), kind=kOutput, calls=%fused_computation.75.clone.1 | convolution fusion | flops 1098909696 | bytes 21505024 | tf_op jit(solution)/shard_map/while/body/eval_jaxpr/sub | solution.py:54
  146.2 8.7 %fusion.70 = bf16[4,512,4,64]{1,3,2,0:T(8,128)(2,1)S(1)} fusion(bf16[4,512,4,64]{1,3,2,0:T(8,128)(2,1)S(1)} %get-tuple-element.179, s32[]{:T(128)} %get-tuple-element.178, bf16[2048,4,64]{0,2,1:T(8,128)(2,1)} %get-tuple-element.198, f32[4,512,2048]{2,1,0:T(8,128)} %get-tuple-element.163, f32[4,512]{1,0:T(4,128)S(1)} %broadcast_select_fusion.4), kind=kOutput, calls=%fused_computation.17.clone.1 | convolution fusion | flops 545390592 | bytes 18096132 | tf_op jit(solution)/shard_map/while/body/eval_jaxpr/hqk,khd->qhd/dot_general | solution.py:58
  157.4 13.4 %fusion.69 = (f32[4,512]{1,0:T(4,128)S(1)}, f32[4,512,2048]{2,1,0:T(8,128)}) fusion(pred[512,2048]{1,0:T(8,128)(4,1)S(1)} %compare_and_fusion.4, bf16[2048,4,64]{0,2,1:T(8,128)(2,1)} %get-tuple-element.197, bf16[2048,4,64]{0,2,1:T(8,128)(2,1)} %get-tuple-element.196, s32[]{:T(128)S(6)} %select_n.104), kind=kOutput, calls=%fused_computation.75.clone.1 | convolution fusion | flops 1098909696 | bytes 21505024 | tf_op jit(solution)/shard_map/while/body/eval_jaxpr/sub | solution.py:54
  170.9 8.7 %fusion.70 = bf16[4,512,4,64]{1,3,2,0:T(8,128)(2,1)S(1)} fusion(bf16[4,512,4,64]{1,3,2,0:T(8,128)(2,1)S(1)} %get-tuple-element.179, s32[]{:T(128)} %get-tuple-element.178, bf16[2048,4,64]{0,2,1:T(8,128)(2,1)} %get-tuple-element.198, f32[4,512,2048]{2,1,0:T(8,128)} %get-tuple-element.163, f32[4,512]{1,0:T(4,128)S(1)} %broadcast_select_fusion.4), kind=kOutput, calls=%fused_computation.17.clone.1 | convolution fusion | flops 545390592 | bytes 18096132 | tf_op jit(solution)/shard_map/while/body/eval_jaxpr/hqk,khd->qhd/dot_general | solution.py:58
  182.1 13.5 %fusion.69 = (f32[4,512]{1,0:T(4,128)S(1)}, f32[4,512,2048]{2,1,0:T(8,128)}) fusion(pred[512,2048]{1,0:T(8,128)(4,1)S(1)} %compare_and_fusion.4, bf16[2048,4,64]{0,2,1:T(8,128)(2,1)} %get-tuple-element.197, bf16[2048,4,64]{0,2,1:T(8,128)(2,1)} %get-tuple-element.196, s32[]{:T(128)S(6)} %select_n.104), kind=kOutput, calls=%fused_computation.75.clone.1 | convolution fusion | flops 1098909696 | bytes 21505024 | tf_op jit(solution)/shard_map/while/body/eval_jaxpr/sub | solution.py:54
  195.6 8.7 %fusion.70 = bf16[4,512,4,64]{1,3,2,0:T(8,128)(2,1)S(1)} fusion(bf16[4,512,4,64]{1,3,2,0:T(8,128)(2,1)S(1)} %get-tuple-element.179, s32[]{:T(128)} %get-tuple-element.178, bf16[2048,4,64]{0,2,1:T(8,128)(2,1)} %get-tuple-element.198, f32[4,512,2048]{2,1,0:T(8,128)} %get-tuple-element.163, f32[4,512]{1,0:T(4,128)S(1)} %broadcast_select_fusion.4), kind=kOutput, calls=%fused_computation.17.clone.1 | convolution fusion | flops 545390592 | bytes 18096132 | tf_op jit(solution)/shard_map/while/body/eval_jaxpr/hqk,khd->qhd/dot_general | solution.py:58
  206.8 13.4 %fusion.69 = (f32[4,512]{1,0:T(4,128)S(1)}, f32[4,512,2048]{2,1,0:T(8,128)}) fusion(pred[512,2048]{1,0:T(8,128)(4,1)S(1)} %compare_and_fusion.4, bf16[2048,4,64]{0,2,1:T(8,128)(2,1)} %get-tuple-element.197, bf16[2048,4,64]{0,2,1:T(8,128)(2,1)} %get-tuple-element.196, s32[]{:T(128)S(6)} %select_n.104), kind=kOutput, calls=%fused_computation.75.clone.1 | convolution fusion | flops 1098909696 | bytes 21505024 | tf_op jit(solution)/shard_map/while/body/eval_jaxpr/sub | solution.py:54
  220.2 8.7 %fusion.70 = bf16[4,512,4,64]{1,3,2,0:T(8,128)(2,1)S(1)} fusion(bf16[4,512,4,64]{1,3,2,0:T(8,128)(2,1)S(1)} %get-tuple-element.179, s32[]{:T(128)} %get-tuple-element.178, bf16[2048,4,64]{0,2,1:T(8,128)(2,1)} %get-tuple-element.198, f32[4,512,2048]{2,1,0:T(8,128)} %get-tuple-element.163, f32[4,512]{1,0:T(4,128)S(1)} %broadcast_select_fusion.4), kind=kOutput, calls=%fused_computation.17.clone.1 | convolution fusion | flops 545390592 | bytes 18096132 | tf_op jit(solution)/shard_map/while/body/eval_jaxpr/hqk,khd->qhd/dot_general | solution.py:58
  230.1 3.3 %convolution_convert_fusion = bf16[2048,1024]{0,1:T(8,128)(2,1)} fusion(bf16[2048,256]{0,1:T(8,128)(2,1)S(1)} %bitcast.50, bf16[256,1024]{1,0:T(8,128)(2,1)S(1)} %copy-done), kind=kOutput, calls=%fused_computation.33 | convolution fusion | flops 1075838976 | bytes 5767168 | tf_op jit(solution)/shard_map/dot_general | solution.py:128
  233.4 5.0 %all-to-all-start.2 = ((bf16[4,2048,256]{1,2,0:T(8,128)(2,1)}), bf16[4,2048,256]{1,2,0:T(8,128)(2,1)}, u32[]{:S(2)}, u32[]{:S(2)}) async-start(bf16[4,2048,256]{1,2,0:T(8,128)(2,1)} %bitcast.47), calls=%async_computation.2 | async-start | bytes 8388608 | tf_op jit(solution)/shard_map/all_to_all | solution.py:19
  239.1 1.4 copy.23
  240.5 44.8 %all-to-all-done.2 = bf16[4,2048,256]{1,2,0:T(8,128)(2,1)} async-done(((bf16[4,2048,256]{1,2,0:T(8,128)(2,1)}), bf16[4,2048,256]{1,2,0:T(8,128)(2,1)}, u32[]{:S(2)}, u32[]{:S(2)}) %all-to-all-start.2) | async-done | bytes 4194336 | tf_op jit(solution)/shard_map/all_to_all | solution.py:19
  285.3 3.2 %convert_reduce_fusion.1 = f32[2048,256]{0,1:T(8,128)S(1)} fusion(bf16[4,2048,256]{1,2,0:T(8,128)(2,1)} %all-to-all-done.2), kind=kLoop, calls=%fused_computation.32 | loop fusion | flops 3670016 | bytes 6291456 | tf_op jit(solution)/shard_map/reduce_sum | solution.py:20
  290.4 12.9 %all-to-all-start.3 = ((f32[64,1,257]{2,1,0:T(1,128)}), f32[64,1,257]{2,1,0:T(1,128)S(1)}, u32[]{:S(2)}, u32[]{:S(2)}) async-start(f32[64,1,257]{2,1,0:T(1,128)} %broadcast_in_dim.134), calls=%async_computation.3 | async-start | bytes 196608 | tf_op jit(solution)/shard_map/all_to_all | solution.py:25
  303.3 2.5 fusion.34
  305.8 2.3 copy.26
  308.1 5.8 %all-to-all-done.3 = f32[64,1,257]{2,1,0:T(1,128)S(1)} async-done(((f32[64,1,257]{2,1,0:T(1,128)}), f32[64,1,257]{2,1,0:T(1,128)S(1)}, u32[]{:S(2)}, u32[]{:S(2)}) %all-to-all-start.3) | async-done | bytes 65824 | tf_op jit(solution)/shard_map/all_to_all | solution.py:25
  (81 shorter events, 19.3 us)
Async XLA Ops:
  7.2 222.9 %copy-start = (bf16[256,1024]{1,0:T(8,128)(2,1)S(1)}, bf16[256,1024]{1,0:T(8,128)(2,1)}, u32[]{:S(2)}) copy-start(bf16[256,1024]{1,0:T(8,128)(2,1)} %param.19) | copy-start | bytes 1572868
  10.3 22.6 %all-to-all-start.1 = ((s32[64,2,1]{1,2,0:T(1,128)}), s32[64,2,1]{1,2,0:T(1,128)S(1)}, u32[]{:S(2)}, u32[]{:S(2)}) async-start(s32[64,2,1]{1,2,0:T(1,128)} %bitcast), calls=%async_computation.1 | async-start | bytes 65536 | tf_op jit(solution)/shard_map/all_to_all | solution.py:96
  26.6 41.1 %copy-start.4 = (s32[128]{0:T(128)S(1)}, s32[128]{0:T(128)}, u32[]{:S(2)}) copy-start(s32[128]{0:T(128)} %param.15) | copy-start | bytes 1540
  32.8 33.1 %all-to-all-start = ((bf16[64,32,256]{2,1,0:T(8,128)(2,1)}), bf16[64,32,256]{2,1,0:T(8,128)(2,1)S(1)}, u32[]{:S(2)}, u32[]{:S(2)}) async-start(bf16[64,32,256]{2,1,0:T(8,128)(2,1)} %bitcast.2), calls=%async_computation | async-start | bytes 2097152 | tf_op jit(solution)/shard_map/all_to_all | solution.py:102
  37.6 79.8 %all-gather.2.cloned.1.call-start = ((), (), s32[]{:S(2)}) async-start(), calls=%async_computation.4 | async-start | bytes 5242880 | tf_op jit(solution)/shard_map/all_gather | solution.py:106
  117.4 3.4 %copy-start.1 = (bf16[2048,1024]{1,0:T(8,128)(2,1)S(1)}, bf16[2048,1024]{1,0:T(8,128)(2,1)}, u32[]{:S(2)}) copy-start(bf16[2048,1024]{1,0:T(8,128)(2,1)} %all-gather.2.cloned.1.call-done) | copy-start | bytes 12582916
  122.2 1.1 copy-start.5
  123.4 2.3 copy-start.6
  125.7 2.3 copy-start.7
  233.4 5.7 %copy-start.2 = (bf16[128,16,256]{2,1,0:T(8,128)(2,1)S(1)}, bf16[128,16,256]{2,1,0:T(8,128)(2,1)}, u32[]{:S(2)}) copy-start(bf16[128,16,256]{2,1,0:T(8,128)(2,1)} %broadcast_select_fusion.1) | copy-start | bytes 3145732
  233.4 51.9 %all-to-all-start.2 = ((bf16[4,2048,256]{1,2,0:T(8,128)(2,1)}), bf16[4,2048,256]{1,2,0:T(8,128)(2,1)}, u32[]{:S(2)}, u32[]{:S(2)}) async-start(bf16[4,2048,256]{1,2,0:T(8,128)(2,1)} %bitcast.47), calls=%async_computation.2 | async-start | bytes 8388608 | tf_op jit(solution)/shard_map/all_to_all | solution.py:19
  285.3 3.3 %copy-start.3 = (bf16[2048,256]{0,1:T(8,128)(2,1)S(1)}, bf16[2048,256]{0,1:T(8,128)(2,1)}, u32[]{:S(2)}) copy-start(bf16[2048,256]{0,1:T(8,128)(2,1)} %copy.23) | copy-start | bytes 3145732
  290.4 23.5 %all-to-all-start.3 = ((f32[64,1,257]{2,1,0:T(1,128)}), f32[64,1,257]{2,1,0:T(1,128)S(1)}, u32[]{:S(2)}, u32[]{:S(2)}) async-start(f32[64,1,257]{2,1,0:T(1,128)} %broadcast_in_dim.134), calls=%async_computation.3 | async-start | bytes 196608 | tf_op jit(solution)/shard_map/all_to_all | solution.py:25
Sparse Core Ops, SparseCore 0:
  67.9 49.4 all-gather.1
where the time goes:
time: 323 us
  waiting for transfers between devices  133 us (41%)
  matrix products  99.3 us (31%)
  starting transfers between devices  35.8 us (11%)
  other arithmetic  22.8 us (7%)
  local copies, waits for them, and re-layouts  14.6 us (5%)
  between operations  14.3 us (4%)
    sub x4, matrix products, attend(): raised = jnp.where(allowed[None], jnp.exp(scores - peak), 0.0)  53.8 us
    all_gather x1, waiting for transfers between devices, on_device(): full_rows = lax.all_gather(own_cols, 'mp', axis=1, tiled=True)  49.4 us
    all_to_all x1, waiting for transfers between devices, sent_and_summed(): lax.all_to_all(cut_along(shard, dim, length), axis, 0, 0, tiled=True)  44.8 us
    dot_general x4, matrix products, attend(): jnp.einsum('hqk,khd->qhd', weights, values, preferred_element_type=jnp.fl...  34.9 us
    all_to_all x1, waiting for transfers between devices, on_device(): lax.all_to_all(outgoing, 'dp', split_axis=0, concat_axis=0, tiled=True)  26.7 us
    all_to_all x1, starting transfers between devices, on_device(): lax.all_to_all(slot_sent, 'dp', split_axis=0, concat_axis=0, tiled=True)  13.1 us
    all_to_all x1, starting transfers between devices, sent_to_all(): return lax.all_to_all(copies, axis, split_axis=0, concat_axis=0, tiled=True)  12.9 us
  transfers between devices with their start and end apart: 5, of which 5 were waited for; matrix products, arithmetic and copies ran while one was open for 4% of the time, Pallas kernels for 0%

commit v1 on v0

--- a/solution.py
+++ b/solution.py
@@ -103,7 +103,7 @@
     own_cols = jnp.take(
         incoming.reshape(slot_count, tile_size, part_width), arrive, axis=0
     ).reshape(slot_count * tile_size, part_width)
-    full_rows = lax.all_gather(own_cols, "mp", axis=1, tiled=True)
+    full_rows = jnp.concatenate(lax.all_gather(own_cols, "mp"), axis=1)
     count_rows = slot_count * tile_size
     segment = jnp.repeat(packed_image, tile_size)
     present = segment >= 0

time: 323 us -> 328 us (1.015)
  local copies, waits for them, and re-layouts: 14.6 us -> 22.5 us
  waiting for transfers between devices: 133 us -> 129 us
    all_gather x0 -> x1, local copies, waits for them, and re-layouts: none -> 6.39 us  [on_device(): full_rows = jnp.concatenate(lax.all_gather(own_cols, 'mp'), axis=1)]
  transfers between devices with their start and end apart: 5 -> 5, of which waited for: 5 -> 5; matrix products, arithmetic and copies ran while one was open for 4% -> 5% of each run, Pallas kernels for 0% -> 0%
where the time goes in v1:
time: 328 us; the launch traced here: 327 us
  waiting for transfers between devices  129 us (39%)
  matrix products  99.4 us (30%)
  starting transfers between devices  34.6 us (11%)
  other arithmetic  24.9 us (8%)
  local copies, waits for them, and re-layouts  22.5 us (7%)
  between operations  14.3 us (4%)
    sub x4, matrix products, attend(): raised = jnp.where(allowed[None], jnp.exp(scores - peak), 0.0)  53.8 us
    all_gather x1, waiting for transfers between devices, on_device(): full_rows = jnp.concatenate(lax.all_gather(own_cols, 'mp'), axis=1)  47.5 us
    all_to_all x1, waiting for transfers between devices, sent_and_summed(): lax.all_to_all(cut_along(shard, dim, length), axis, 0, 0, tiled=True)  42.9 us
    dot_general x4, matrix products, attend(): jnp.einsum('hqk,khd->qhd', weights, values, preferred_element_type=jnp.fl...  34.9 us
    all_to_all x1, waiting for transfers between devices, on_device(): lax.all_to_all(outgoing, 'dp', split_axis=0, concat_axis=0, tiled=True)  26.7 us
    all_to_all x1, starting transfers between devices, on_device(): lax.all_to_all(slot_sent, 'dp', split_axis=0, concat_axis=0, tiled=True)  13.1 us
    all_to_all x1, starting transfers between devices, sent_to_all(): return lax.all_to_all(copies, axis, split_axis=0, concat_axis=0, tiled=True)  11.7 us
  transfers between devices with their start and end apart: 5, of which 5 were waited for; matrix products, arithmetic and copies ran while one was open for 5% of the time, Pallas kernels for 0%

profile of v1, /device:TPU:1, one launch (start us, length us, event | category | flops | bytes accessed | tf_op | source)
XLA Modules:
  0.0 327.3 jit_solution(7081364711058602366)
XLA Ops:
  10.3 13.1 %all-to-all-start.1 = ((s32[64,2,1]{1,2,0:T(1,128)}), s32[64,2,1]{1,2,0:T(1,128)S(1)}, u32[]{:S(2)}, u32[]{:S(2)}) async-start(s32[64,2,1]{1,2,0:T(1,128)} %bitcast), calls=%async_computation.1 | async-start | bytes 65536 | tf_op jit(solution)/shard_map/all_to_all | solution.py:96
  23.5 1.3 constant_dynamic-slice_fusion
  25.4 1.2 broadcast_select_fusion.2
  26.6 6.2 %all-to-all-done.1 = s32[64,2,1]{1,2,0:T(1,128)S(1)} async-done(((s32[64,2,1]{1,2,0:T(1,128)}), s32[64,2,1]{1,2,0:T(1,128)S(1)}, u32[]{:S(2)}, u32[]{:S(2)}) %all-to-all-start.1) | async-done | bytes 544 | tf_op jit(solution)/shard_map/all_to_all | solution.py:96
  32.8 4.7 %all-to-all-start = ((bf16[64,32,256]{2,1,0:T(8,128)(2,1)}), bf16[64,32,256]{2,1,0:T(8,128)(2,1)S(1)}, u32[]{:S(2)}, u32[]{:S(2)}) async-start(bf16[64,32,256]{2,1,0:T(8,128)(2,1)} %bitcast.2), calls=%async_computation | async-start | bytes 2097152 | tf_op jit(solution)/shard_map/all_to_all | solution.py:102
  39.2 26.7 %all-to-all-done = bf16[64,32,256]{2,1,0:T(8,128)(2,1)S(1)} async-done(((bf16[64,32,256]{2,1,0:T(8,128)(2,1)}), bf16[64,32,256]{2,1,0:T(8,128)(2,1)S(1)}, u32[]{:S(2)}, u32[]{:S(2)}) %all-to-all-start) | async-done | bytes 1048608 | tf_op jit(solution)/shard_map/all_to_all | solution.py:102
  67.9 47.5 %all-gather.2.cloned.1.call-done = bf16[4,2048,256]{2,1,0:T(8,128)(2,1)} async-done(((bf16[1,2048,256]{2,1,0:T(8,128)(2,1)}), bf16[4,2048,256]{2,1,0:T(8,128)(2,1)}) %all-gather.2.cloned.1.call-update) | async-done | bytes 4194320 | tf_op jit(solution)/shard_map/all_gather | solution.py:106
  115.4 6.4 %copy.25 = bf16[4,2048,256]{1,2,0:T(8,128)(2,1)} copy(bf16[4,2048,256]{2,1,0:T(8,128)(2,1)} %all-gather.2.cloned.1.call-done) | data formatting | bytes 8388608 | tf_op jit(solution)/shard_map/all_gather | solution.py:106
  121.8 3.0 convert_reduce_fusion.1
  126.4 1.4 fusion.30
  127.9 2.3 convolution_convert_fusion.1
  130.2 2.3 convolution_convert_fusion.3
  132.5 2.3 convolution_convert_fusion.2
  134.9 98.7 %while.11 = (s32[]{:T(128)}, bf16[4,512,4,64]{1,3,2,0:T(8,128)(2,1)S(1)}, s32[4]{0:T(128)S(1)}, s32[2048]{0:T(1024)S(1)}, pred[2048]{0:T(1024)(128)(4,1)S(1)}, /...) while((s32[]{:T(128)}, ...), condition=%wide.region_9.11_spmd.clone, body=%wide.region_6.0_spmd.clone.sunk | while | flops 1646399488 | bytes 40707776 | solution.py:75
  137.3 13.4 %fusion.63 = (f32[4,512]{1,0:T(4,128)S(1)}, f32[4,512,2048]{2,1,0:T(8,128)}) fusion(pred[512,2048]{1,0:T(8,128)(4,1)S(1)} %compare_and_fusion.4, bf16[2048,4,64]{0,2,1:T(8,128)(2,1)} %get-tuple-element.195, bf16[2048,4,64]{0,2,1:T(8,128)(2,1)} %get-tuple-element.194, s32[]{:T(128)S(6)} %select_n.102), kind=kOutput, calls=%fused_computation.72.clone.1 | convolution fusion | flops 1098909696 | bytes 21505024 | tf_op jit(solution)/shard_map/while/body/eval_jaxpr/sub | solution.py:54
  150.8 8.7 %fusion.64 = bf16[4,512,4,64]{1,3,2,0:T(8,128)(2,1)S(1)} fusion(bf16[4,512,4,64]{1,3,2,0:T(8,128)(2,1)S(1)} %get-tuple-element.177, s32[]{:T(128)} %get-tuple-element.176, bf16[2048,4,64]{0,2,1:T(8,128)(2,1)} %get-tuple-element.196, f32[4,512,2048]{2,1,0:T(8,128)} %get-tuple-element.161, f32[4,512]{1,0:T(4,128)S(1)} %broadcast_select_fusion.4), kind=kOutput, calls=%fused_computation.17.clone.1 | convolution fusion | flops 545390592 | bytes 18096132 | tf_op jit(solution)/shard_map/while/body/eval_jaxpr/hqk,khd->qhd/dot_general | solution.py:58
  162.0 13.4 %fusion.63 = (f32[4,512]{1,0:T(4,128)S(1)}, f32[4,512,2048]{2,1,0:T(8,128)}) fusion(pred[512,2048]{1,0:T(8,128)(4,1)S(1)} %compare_and_fusion.4, bf16[2048,4,64]{0,2,1:T(8,128)(2,1)} %get-tuple-element.195, bf16[2048,4,64]{0,2,1:T(8,128)(2,1)} %get-tuple-element.194, s32[]{:T(128)S(6)} %select_n.102), kind=kOutput, calls=%fused_computation.72.clone.1 | convolution fusion | flops 1098909696 | bytes 21505024 | tf_op jit(solution)/shard_map/while/body/eval_jaxpr/sub | solution.py:54
  175.4 8.7 %fusion.64 = bf16[4,512,4,64]{1,3,2,0:T(8,128)(2,1)S(1)} fusion(bf16[4,512,4,64]{1,3,2,0:T(8,128)(2,1)S(1)} %get-tuple-element.177, s32[]{:T(128)} %get-tuple-element.176, bf16[2048,4,64]{0,2,1:T(8,128)(2,1)} %get-tuple-element.196, f32[4,512,2048]{2,1,0:T(8,128)} %get-tuple-element.161, f32[4,512]{1,0:T(4,128)S(1)} %broadcast_select_fusion.4), kind=kOutput, calls=%fused_computation.17.clone.1 | convolution fusion | flops 545390592 | bytes 18096132 | tf_op jit(solution)/shard_map/while/body/eval_jaxpr/hqk,khd->qhd/dot_general | solution.py:58
  186.6 13.5 %fusion.63 = (f32[4,512]{1,0:T(4,128)S(1)}, f32[4,512,2048]{2,1,0:T(8,128)}) fusion(pred[512,2048]{1,0:T(8,128)(4,1)S(1)} %compare_and_fusion.4, bf16[2048,4,64]{0,2,1:T(8,128)(2,1)} %get-tuple-element.195, bf16[2048,4,64]{0,2,1:T(8,128)(2,1)} %get-tuple-element.194, s32[]{:T(128)S(6)} %select_n.102), kind=kOutput, calls=%fused_computation.72.clone.1 | convolution fusion | flops 1098909696 | bytes 21505024 | tf_op jit(solution)/shard_map/while/body/eval_jaxpr/sub | solution.py:54
  200.1 8.7 %fusion.64 = bf16[4,512,4,64]{1,3,2,0:T(8,128)(2,1)S(1)} fusion(bf16[4,512,4,64]{1,3,2,0:T(8,128)(2,1)S(1)} %get-tuple-element.177, s32[]{:T(128)} %get-tuple-element.176, bf16[2048,4,64]{0,2,1:T(8,128)(2,1)} %get-tuple-element.196, f32[4,512,2048]{2,1,0:T(8,128)} %get-tuple-element.161, f32[4,512]{1,0:T(4,128)S(1)} %broadcast_select_fusion.4), kind=kOutput, calls=%fused_computation.17.clone.1 | convolution fusion | flops 545390592 | bytes 18096132 | tf_op jit(solution)/shard_map/while/body/eval_jaxpr/hqk,khd->qhd/dot_general | solution.py:58
  211.4 13.4 %fusion.63 = (f32[4,512]{1,0:T(4,128)S(1)}, f32[4,512,2048]{2,1,0:T(8,128)}) fusion(pred[512,2048]{1,0:T(8,128)(4,1)S(1)} %compare_and_fusion.4, bf16[2048,4,64]{0,2,1:T(8,128)(2,1)} %get-tuple-element.195, bf16[2048,4,64]{0,2,1:T(8,128)(2,1)} %get-tuple-element.194, s32[]{:T(128)S(6)} %select_n.102), kind=kOutput, calls=%fused_computation.72.clone.1 | convolution fusion | flops 1098909696 | bytes 21505024 | tf_op jit(solution)/shard_map/while/body/eval_jaxpr/sub | solution.py:54
  224.8 8.7 %fusion.64 = bf16[4,512,4,64]{1,3,2,0:T(8,128)(2,1)S(1)} fusion(bf16[4,512,4,64]{1,3,2,0:T(8,128)(2,1)S(1)} %get-tuple-element.177, s32[]{:T(128)} %get-tuple-element.176, bf16[2048,4,64]{0,2,1:T(8,128)(2,1)} %get-tuple-element.196, f32[4,512,2048]{2,1,0:T(8,128)} %get-tuple-element.161, f32[4,512]{1,0:T(4,128)S(1)} %broadcast_select_fusion.4), kind=kOutput, calls=%fused_computation.17.clone.1 | convolution fusion | flops 545390592 | bytes 18096132 | tf_op jit(solution)/shard_map/while/body/eval_jaxpr/hqk,khd->qhd/dot_general | solution.py:58
  234.6 3.3 %convolution_convert_fusion = bf16[2048,1024]{0,1:T(8,128)(2,1)} fusion(bf16[2048,256]{0,1:T(8,128)(2,1)S(1)} %bitcast.60, bf16[256,1024]{1,0:T(8,128)(2,1)S(1)} %copy-done), kind=kOutput, calls=%fused_computation.32 | convolution fusion | flops 1075838976 | bytes 5767168 | tf_op jit(solution)/shard_map/dot_general | solution.py:128
  237.9 5.0 %all-to-all-start.2 = ((bf16[4,2048,256]{1,2,0:T(8,128)(2,1)}), bf16[4,2048,256]{1,2,0:T(8,128)(2,1)}, u32[]{:S(2)}, u32[]{:S(2)}) async-start(bf16[4,2048,256]{1,2,0:T(8,128)(2,1)} %bitcast.58), calls=%async_computation.2 | async-start | bytes 8388608 | tf_op jit(solution)/shard_map/all_to_all | solution.py:19
  243.7 1.5 bitcast_convert_fusion
  245.2 3.0 copy.27
  248.1 42.9 %all-to-all-done.2 = bf16[4,2048,256]{1,2,0:T(8,128)(2,1)} async-done(((bf16[4,2048,256]{1,2,0:T(8,128)(2,1)}), bf16[4,2048,256]{1,2,0:T(8,128)(2,1)}, u32[]{:S(2)}, u32[]{:S(2)}) %all-to-all-start.2) | async-done | bytes 4194336 | tf_op jit(solution)/shard_map/all_to_all | solution.py:19
  291.0 3.3 %convert_reduce_fusion = f32[2048,256]{0,1:T(8,128)S(1)} fusion(bf16[4,2048,256]{1,2,0:T(8,128)(2,1)} %all-to-all-done.2), kind=kLoop, calls=%fused_computation.29 | loop fusion | flops 3670016 | bytes 6291456 | tf_op jit(solution)/shard_map/reduce_sum | solution.py:20
  296.2 11.7 %all-to-all-start.3 = ((f32[64,1,257]{2,1,0:T(1,128)}), f32[64,1,257]{2,1,0:T(1,128)S(1)}, u32[]{:S(2)}, u32[]{:S(2)}) async-start(f32[64,1,257]{2,1,0:T(1,128)} %broadcast_in_dim.134), calls=%async_computation.3 | async-start | bytes 196608 | tf_op jit(solution)/shard_map/all_to_all | solution.py:25
  307.9 3.0 fusion.31
  310.9 2.3 copy.29
  313.2 5.4 %all-to-all-done.3 = f32[64,1,257]{2,1,0:T(1,128)S(1)} async-done(((f32[64,1,257]{2,1,0:T(1,128)}), f32[64,1,257]{2,1,0:T(1,128)S(1)}, u32[]{:S(2)}, u32[]{:S(2)}) %all-to-all-start.3) | async-done | bytes 65824 | tf_op jit(solution)/shard_map/all_to_all | solution.py:25
  (83 shorter events, 21.6 us)
Async XLA Ops:
  7.2 227.5 %copy-start = (bf16[256,1024]{1,0:T(8,128)(2,1)S(1)}, bf16[256,1024]{1,0:T(8,128)(2,1)}, u32[]{:S(2)}) copy-start(bf16[256,1024]{1,0:T(8,128)(2,1)} %param.19) | copy-start | bytes 1572868
  10.3 22.6 %all-to-all-start.1 = ((s32[64,2,1]{1,2,0:T(1,128)}), s32[64,2,1]{1,2,0:T(1,128)S(1)}, u32[]{:S(2)}, u32[]{:S(2)}) async-start(s32[64,2,1]{1,2,0:T(1,128)} %bitcast), calls=%async_computation.1 | async-start | bytes 65536 | tf_op jit(solution)/shard_map/all_to_all | solution.py:96
  26.6 41.1 %copy-start.4 = (s32[128]{0:T(128)S(1)}, s32[128]{0:T(128)}, u32[]{:S(2)}) copy-start(s32[128]{0:T(128)} %param.15) | copy-start | bytes 1540
  32.8 33.1 %all-to-all-start = ((bf16[64,32,256]{2,1,0:T(8,128)(2,1)}), bf16[64,32,256]{2,1,0:T(8,128)(2,1)S(1)}, u32[]{:S(2)}, u32[]{:S(2)}) async-start(bf16[64,32,256]{2,1,0:T(8,128)(2,1)} %bitcast.2), calls=%async_computation | async-start | bytes 2097152 | tf_op jit(solution)/shard_map/all_to_all | solution.py:102
  37.6 77.8 %all-gather.2.cloned.1.call-start = ((), (), s32[]{:S(2)}) async-start(), calls=%async_computation.4 | async-start | bytes 5242880 | tf_op jit(solution)/shard_map/all_gather | solution.py:106
  121.8 3.4 %copy-start.1 = (bf16[4,2048,256]{1,2,0:T(8,128)(2,1)S(1)}, bf16[4,2048,256]{1,2,0:T(8,128)(2,1)}, u32[]{:S(2)}) copy-start(bf16[4,2048,256]{1,2,0:T(8,128)(2,1)} %copy.25) | copy-start | bytes 12582916
  126.4 1.5 copy-start.5
  127.9 2.3 copy-start.6
  130.2 2.3 copy-start.7
  237.9 5.7 %copy-start.3 = (bf16[128,16,256]{2,1,0:T(8,128)(2,1)S(1)}, bf16[128,16,256]{2,1,0:T(8,128)(2,1)}, u32[]{:S(2)}) copy-start(bf16[128,16,256]{2,1,0:T(8,128)(2,1)} %broadcast_select_fusion.1) | copy-start | bytes 3145732
  237.9 53.1 %all-to-all-start.2 = ((bf16[4,2048,256]{1,2,0:T(8,128)(2,1)}), bf16[4,2048,256]{1,2,0:T(8,128)(2,1)}, u32[]{:S(2)}, u32[]{:S(2)}) async-start(bf16[4,2048,256]{1,2,0:T(8,128)(2,1)} %bitcast.58), calls=%async_computation.2 | async-start | bytes 8388608 | tf_op jit(solution)/shard_map/all_to_all | solution.py:19
  291.0 3.3 %copy-start.2 = (f32[2048,256]{0,1:T(8,128)S(1)}, f32[2048,256]{0,1:T(8,128)}, u32[]{:S(2)}) copy-start(f32[2048,256]{0,1:T(8,128)} %copy.27) | copy-start | bytes 6291460
  296.2 22.3 %all-to-all-start.3 = ((f32[64,1,257]{2,1,0:T(1,128)}), f32[64,1,257]{2,1,0:T(1,128)S(1)}, u32[]{:S(2)}, u32[]{:S(2)}) async-start(f32[64,1,257]{2,1,0:T(1,128)} %broadcast_in_dim.134), calls=%async_computation.3 | async-start | bytes 196608 | tf_op jit(solution)/shard_map/all_to_all | solution.py:25
Sparse Core Ops, SparseCore 0:
  67.9 47.4 all-gather.1
